TPU v7x, 32 devices: a whole 2x2x4 slice. The times are simulated.
32 devices in a mesh: gx: 8 (over z, y), yz: 4 (over x, core).
Axes of the slice: x: 2, y: 2, z: 4, core: 2. Of those that a mesh axis runs over, the one named last changes fastest.
Arguments:
- solvent_vel: float32 [3, 256, 128, 2, 128], P(None, 'gx', 'yz'), may hold values from -6 to 6
- occupancy: int32 [256, 128, 128], P('gx', 'yz'), may hold values from 0 to 2
- grid_shift: int32 [3], replicated, may hold values from 1 to 3
- axis_index: int32 [64, 32, 64], P('gx', 'yz'), may hold values from 0 to 63
- colloid_pos: float32 [3, 8, 4, 128], P(None, 'gx', 'yz'), may hold values from 0 to 64, as said below
- colloid_vel: float32 [3, 8, 4, 128], P(None, 'gx', 'yz'), may hold values from -6 to 6
- colloid_mass: float32 [8, 4, 128], P('gx', 'yz'), may hold values from 2 to 20
- colloid_count: int32 [8, 4], P('gx', 'yz'), may hold values from 21 to 128, as said below
Outputs:
- solvent_out: float32 [3, 256, 128, 2, 128], P(None, 'gx', 'yz')
- colloid_pos_out: float32 [3, 8, 4, 128], P(None, 'gx', 'yz')
- colloid_vel_out: float32 [3, 8, 4, 128], P(None, 'gx', 'yz')
Inputs may be any that keep to these rules, and one draw needn't show every extreme that they name: `colloid_pos`: component 0 lies in [0, 8), component 1 in [0, 8), component 2 in [0, 64). `colloid_count`: some device holds 128 live colloids in every draw.
All inputs are finite; a program needn't handle non-finite values.
Results may differ from a plain program's by a relative error of at most 0.0003.
Values sent between devices are 32-bit elements; how exact they have to be, the bound alone decides.
A program may use at most 320 MiB of HBM per device.

v0:
```python
import functools
import math

import jax
import jax.numpy as jnp
from jax import lax
from jax.experimental import pallas as pl
from jax.experimental.pallas import tpu as pltpu
from jax.sharding import PartitionSpec as P

CX = 8
CY = 8
CZ = 64
SUB = 4
SUBSTEPS = 4
DIRECTIONS = 64


turn_angle = 130.0 * math.pi / 180.0
cos_angle = math.cos(turn_angle)
sin_angle = math.sin(turn_angle)
golden = math.pi * (3.0 - math.sqrt(5.0))
cutoff = 1.5
stiffness = 20.0
timestep = 0.05
fill_mass = 16.0
MESH = pl.DeviceIdType.MESH


def iota(shape, dim):
    return lax.broadcasted_iota(jnp.int32, shape, dim)


def three_terms(value):
    high = value.astype(jnp.bfloat16)
    rest = value - high.astype(jnp.float32)
    middle = rest.astype(jnp.bfloat16)
    low = (rest - middle.astype(jnp.float32)).astype(jnp.bfloat16)
    return (high, middle, low)


def dot(left, right, contract=((1,), (0,))):
    return lax.dot_general(left, right, (contract, ((), ())), preferred_element_type=jnp.float32)


def wrapped(value, size):
    return jnp.where(value >= size, value - size, value)


def layer_of(row, scale, width):
    return jnp.clip(jnp.floor(row * scale).astype(jnp.int32), 0, width - 1)


def sums_kernel(shape, steps, shift, count, solvent, occupancy, pos, vel, mass, out, acc):
    width_x, width_y, width_z = shape
    cells_x, cells_y = (width_x // SUB + 1, width_y // SUB + 1)
    block_x = width_x // steps
    rows = 2 * width_y
    step = pl.program_id(0)
    shift_x, shift_y, shift_z = (shift[0], shift[1], shift[2])

    @pl.when(step == 0)
    def _():
        acc[...] = jnp.zeros_like(acc)

    double = (iota((rows, width_y), 0) >> 1 == iota((rows, width_y), 1)).astype(jnp.bfloat16)
    slot = (iota((rows, width_z), 0) & 1).astype(jnp.float32)
    for x in range(block_x):
        filled = occupancy[x].astype(jnp.float32)
        live = dot(double, filled.astype(jnp.bfloat16)) > slot
        cell = (step * block_x + x + shift_x) >> 2
        for c in range(3):
            at = pl.ds(c * rows, rows)
            acc[cell, at, :] += jnp.where(live, solvent[c, x], 0.0)
        acc[cell, pl.ds(3 * rows, width_y), :] += filled

    @pl.when(step == steps - 1)
    def _():
        total = 3 * rows + width_y
        column = iota((cells_y * 8, total), 1)
        target = iota((cells_y * 8, total), 0)
        heavy = column >= 3 * rows
        part = jnp.where(heavy, 3, (column >= rows).astype(jnp.int32) + (column >= 2 * rows).astype(jnp.int32))
        layer = jnp.where(heavy, column - 3 * rows, (column - part * rows) >> 1)
        fits = jnp.logical_and(part == (target & 7), ((layer + shift_y) >> 2) == (target >> 3))
        select = fits.astype(jnp.float32).astype(jnp.bfloat16)

        cell_x = (layer_of(pos[0, 0], SUB, width_x) + shift_x) >> 2
        cell_y = (layer_of(pos[1, 0], SUB, width_y) + shift_y) >> 2
        cell_z = wrapped(layer_of(pos[2, 0], 2.0, width_z) + shift_z, width_z) >> 1
        slots = mass.shape[2]
        alive = (iota((1, slots), 1) < count[0, 0]).astype(jnp.float32)
        weight = mass[0] * alive
        comp = iota((8, slots), 0)
        values = jnp.where(
            comp == 0,
            vel[0, 0] * weight,
            jnp.where(
                comp == 1,
                vel[1, 0] * weight,
                jnp.where(comp == 2, vel[2, 0] * weight, jnp.where(comp == 3, weight, 0.0)),
            ),
        )
        place = jnp.broadcast_to(cell_x * cells_y + cell_y, (8, slots))
        near = (wrapped(iota((width_z, slots), 0) + shift_z, width_z) >> 1) == cell_z
        near = near.astype(jnp.float32).astype(jnp.bfloat16)
        even = ((iota((cells_y * 8, width_z), 1) + shift_z) & 1) == 0
        for i in range(cells_x):
            sums = sum(dot(select, term) for term in three_terms(acc[i])[::-1])
            partner = jnp.where(
                even, pltpu.roll(sums, width_z - 1, 1), pltpu.roll(sums, 1, 1)
            )
            number = iota((cells_y, 8, slots), 0) + i * cells_y
            spread = jnp.where(number == place[None], values[None], 0.0).reshape(cells_y * 8, slots)
            deposit = sum(dot(term, near, ((1,), (1,))) for term in three_terms(spread)[::-1])
            out[i] = (sums + partner + deposit).reshape(cells_y, 8, width_z)


def exchange_kernel(
    shape, shift, count, part, axis, pos, vel, mass, fields, pos_out, vel_out,
    halo_x, halo_y, halo_c, edge_x, edge_y, edge_c, sent, got, own, force,
    halo_sem, edge_sem, sent_sem, got_sem,
):
    width_x, width_y, width_z = shape
    n_x, n_y = (width_x // SUB, width_y // SUB)
    slots = mass.shape[2]
    me_x, me_y = (lax.axis_index("gx"), lax.axis_index("yz"))
    size_x, size_y = (lax.axis_size("gx"), lax.axis_size("yz"))
    shift_x, shift_y, shift_z = (shift[0], shift[1], shift[2])

    def device(a, b):
        return (lax.rem(me_x + a + size_x, size_x), lax.rem(me_y + b + size_y, size_y))

    around = [(a, b) for a in (-1, 0, 1) for b in (-1, 0, 1) if (a, b) != (0, 0)]
    barrier = pltpu.get_barrier_semaphore()
    for a, b in around:
        pl.semaphore_signal(barrier, inc=1, device_id=device(a, b), device_id_type=MESH)

    alive = (iota((1, slots), 1) < count[0, 0]).astype(jnp.float32)
    comp = iota((8, slots), 0)

    def stacked(rows):
        out = jnp.zeros((8, slots), jnp.float32)
        for c, row in enumerate(rows):
            out = jnp.where(comp == c, row, out)
        return out

    def columns(rows):
        block = jnp.concatenate([rows, jnp.zeros((slots - 8, slots), jnp.float32)], axis=0)
        return block.T

    start_rows = stacked([pos[0, 0], pos[1, 0], pos[2, 0], alive, mass[0]])
    sent[0] = start_rows
    pl.semaphore_wait(barrier, len(around))

    def remote(src, dst, send, receive, where):
        return pltpu.make_async_remote_copy(
            src_ref=src, dst_ref=dst, send_sem=send, recv_sem=receive,
            device_id=where, device_id_type=MESH,
        )

    halo = [
        remote(part.at[n_x, pl.ds(0, n_y)], halo_x, halo_sem.at[0], halo_sem.at[3], device(1, 0)),
        remote(part.at[pl.ds(0, n_x), n_y], halo_y, halo_sem.at[1], halo_sem.at[4], device(0, 1)),
        remote(part.at[n_x, n_y], halo_c, halo_sem.at[2], halo_sem.at[5], device(1, 1)),
    ]
    for copy in halo:
        copy.start()

    def exchange(step):
        copies = []
        for k, (a, b) in enumerate(around):
            copies.append(
                remote(
                    sent.at[step], got.at[step, 7 - k],
                    sent_sem.at[step, k], got_sem.at[step, 7 - k], device(a, b),
                )
            )
        for copy in copies:
            copy.start()
        return copies

    copies = exchange(0)

    state = columns(start_rows)
    place = [state[:, c : c + 1] for c in range(3)]
    mass_column = state[:, 4:5]

    index = axis[...].reshape(n_x * n_y, width_z // 2).astype(jnp.float32).astype(jnp.bfloat16)
    cell_z = wrapped(iota((width_z // 2, width_z), 1) + shift_z, width_z) >> 1
    expand = (cell_z == iota((width_z // 2, width_z), 0)).astype(jnp.float32).astype(jnp.bfloat16)
    number = dot(index, expand)
    height = 1.0 - (2.0 * number + 1.0) / DIRECTIONS
    radius = jnp.sqrt(1.0 - height * height)
    phase = number * golden
    normal = [radius * jnp.cos(phase), radius * jnp.sin(phase), height]
    sub = iota((n_x * n_y, 8, width_z), 1)
    spread = [jnp.broadcast_to(n[:, None, :], (n_x * n_y, 8, width_z)) for n in normal]
    directions = jnp.where(sub == 3, spread[0], jnp.where(sub == 4, spread[1], spread[2]))
    fields[pl.ds(0, n_x), pl.ds(0, n_y)] = directions.reshape(n_x, n_y, 8, width_z)

    for copy in halo:
        copy.wait()
    sub = iota((n_y, 8, width_z), 1)
    for i in range(n_x):
        total = part[i, pl.ds(0, n_y)]
        first = halo_y[i][None]
        if i == 0:
            total = total + halo_x[...]
            first = first + halo_c[...][None]
        total = jnp.concatenate([total[:1] + first, total[1:]], axis=0)
        mean = total / jnp.maximum(total[:, 3:4, :], fill_mass)
        fields[i, pl.ds(0, n_y)] = jnp.where(sub < 3, mean, fields[i, pl.ds(0, n_y)])
    edges = [
        remote(fields.at[0, pl.ds(0, n_y)], edge_x, edge_sem.at[0], edge_sem.at[3], device(-1, 0)),
        remote(fields.at[pl.ds(0, n_x), 0], edge_y, edge_sem.at[1], edge_sem.at[4], device(0, -1)),
        remote(fields.at[0, 0], edge_c, edge_sem.at[2], edge_sem.at[5], device(-1, -1)),
    ]
    for copy in edges:
        copy.start()

    def forces(step, copies, place):
        for c in range(3):
            own[c] = jnp.broadcast_to(place[c], (slots, slots))
        for copy in copies:
            copy.wait()

        def block(r, carry):
            at = pl.ds(pl.multiple_of(r * 8, 8), 8)
            own_x, own_y, own_z = (own[0, at, :], own[1, at, :], own[2, at, :])
            total = [jnp.zeros((8, slots), jnp.float32)] * 3
            sources = [((0, 0), None)] + [(pair, k) for k, pair in enumerate(around)]
            for (a, b), k in sources:
                def row(c):
                    if k is None:
                        return sent[step, pl.ds(c, 1), :]
                    return got[step, k, pl.ds(c, 1), :]

                diff_x = own_x - (row(0) + float(a * CX))
                diff_y = own_y - (row(1) + float(b * CY))
                high = own_z - row(2)
                high = jnp.where(
                    high > 0.5 * CZ, high - CZ, jnp.where(high < -0.5 * CZ, high + CZ, high)
                )
                radius_sq = diff_x * diff_x + diff_y * diff_y + high * high
                reach = 1.0 - radius_sq * (1.0 / (cutoff * cutoff))
                weight = jnp.where(radius_sq < cutoff * cutoff, reach * reach, 0.0) * row(3)
                total = [
                    total[0] + weight * diff_x,
                    total[1] + weight * diff_y,
                    total[2] + weight * high,
                ]
            for c in range(3):
                force[c, at, :] = total[c]
            return carry

        lax.fori_loop(0, slots // 8, block, 0)
        return [stiffness * jnp.sum(force[c], axis=1, keepdims=True) for c in range(3)]

    push = forces(0, copies, place)

    for copy in edges:
        copy.wait()
    fields[n_x, pl.ds(0, n_y)] = edge_x[...]
    fields[pl.ds(0, n_x), n_y] = edge_y[...]
    fields[n_x, n_y] = edge_c[...]

    layer_z = layer_of(pos[2, 0], 2.0, width_z)
    cell_x = (layer_of(pos[0, 0], SUB, width_x) + shift_x) >> 2
    cell_y = (layer_of(pos[1, 0], SUB, width_y) + shift_y) >> 2
    target = jnp.broadcast_to(cell_x * (n_y + 1) + cell_y, (8, slots))
    chosen = (iota((width_z, slots), 0) == layer_z).astype(jnp.float32).astype(jnp.bfloat16)
    picked = jnp.zeros((8, slots), jnp.float32)
    for i in range(n_x + 1):
        rows = fields[i].reshape((n_y + 1) * 8, width_z)
        at_z = sum(dot(term, chosen) for term in three_terms(rows)[::-1])
        number = iota((n_y + 1, 8, slots), 0) + i * (n_y + 1)
        at_z = at_z.reshape(n_y + 1, 8, slots)
        picked = picked + jnp.sum(jnp.where(number == target[None], at_z, 0.0), axis=0)
    mean = [picked[c : c + 1] for c in range(3)]
    n = [picked[c : c + 1] for c in range(3, 6)]
    rel = [vel[c, 0] - mean[c] for c in range(3)]
    cross = [n[1] * rel[2] - n[2] * rel[1], n[2] * rel[0] - n[0] * rel[2], n[0] * rel[1] - n[1] * rel[0]]
    along = n[0] * rel[0] + n[1] * rel[1] + n[2] * rel[2]
    turned = [
        mean[c] + cos_angle * rel[c] + sin_angle * cross[c] + (1.0 - cos_angle) * along * n[c]
        for c in range(3)
    ]
    state = columns(stacked([jnp.where(alive > 0, turned[c], vel[c, 0]) for c in range(3)]))
    speed = [state[:, c : c + 1] for c in range(3)]

    lane = iota((slots, slots), 1)
    for step in range(SUBSTEPS):
        speed = [speed[c] + timestep * push[c] / mass_column for c in range(3)]
        place = [place[c] + timestep * speed[c] for c in range(3)]
        block = jnp.zeros((slots, slots), jnp.float32)
        for c, column in enumerate(place):
            block = jnp.where(lane == c, column, block)
        if step == SUBSTEPS - 1:
            for c, column in enumerate(speed):
                block = jnp.where(lane == 3 + c, column, block)
        flipped = block.T[:8]
        if step < SUBSTEPS - 1:
            sent[step + 1] = jnp.where(comp == 3, alive, flipped)
            copies = exchange(step + 1)
            push = forces(step + 1, copies, place)
    for c in range(3):
        pos_out[c, 0] = jnp.where(alive > 0, flipped[c : c + 1], pos[c, 0])
        vel_out[c, 0] = jnp.where(alive > 0, flipped[3 + c : 4 + c], vel[c, 0])


def rotate_kernel(shape, steps, shift, solvent, occupancy, fields, out):
    width_x, width_y, width_z = shape
    block_x = width_x // steps
    n_y = width_y // SUB
    rows = 2 * width_y
    step = pl.program_id(0)
    shift_x, shift_y = (shift[0], shift[1])
    double = (iota((rows, width_y), 0) >> 1 == iota((rows, width_y), 1)).astype(jnp.bfloat16)
    row = iota((8, width_z), 0)
    slot = (row & 1).astype(jnp.float32)
    later = ((row >> 1) + shift_y) >= SUB

    def layer(x, carry):
        held = dot(double, occupancy[x].astype(jnp.float32).astype(jnp.bfloat16))
        cell = (step * block_x + x + shift_x) >> 2
        for b in range(n_y):
            at = pl.ds(8 * b, 8)
            both = [
                jnp.where(
                    later, fields[cell, b + 1, pl.ds(c, 1), :], fields[cell, b, pl.ds(c, 1), :]
                )
                for c in range(6)
            ]
            mean, n = (both[:3], both[3:])
            old = [solvent[c, x, at, :] for c in range(3)]
            rel = [old[c] - mean[c] for c in range(3)]
            along = (1.0 - cos_angle) * (n[0] * rel[0] + n[1] * rel[1] + n[2] * rel[2])
            cross = [
                n[1] * rel[2] - n[2] * rel[1],
                n[2] * rel[0] - n[0] * rel[2],
                n[0] * rel[1] - n[1] * rel[0],
            ]
            live = held[8 * b : 8 * b + 8] > slot
            for c in range(3):
                new = mean[c] + cos_angle * rel[c] + sin_angle * cross[c] + along * n[c]
                out[c, x, at, :] = jnp.where(live, new, old[c])
        return carry

    lax.fori_loop(0, block_x, layer, 0)


def per_device(
    solvent_vel,
    occupancy,
    grid_shift,
    axis_index,
    colloid_pos,
    colloid_vel,
    colloid_mass,
    colloid_count,
):
    shape = occupancy.shape
    width_x, width_y, width_z = shape
    rows = 2 * width_y
    n_x, n_y = (width_x // SUB, width_y // SUB)
    slots = colloid_mass.shape[2]
    steps = 4
    block_x = width_x // steps
    solvent = solvent_vel.reshape(3, width_x, rows, width_z)
    smem = pl.BlockSpec(memory_space=pltpu.SMEM)
    vmem = pl.BlockSpec(memory_space=pltpu.VMEM)
    solvent_spec = pl.BlockSpec((3, block_x, rows, width_z), lambda i: (0, i, 0, 0))
    occupancy_spec = pl.BlockSpec((block_x, width_y, width_z), lambda i: (i, 0, 0))
    cells = (n_x + 1, n_y + 1, 8, width_z)
    f32 = jnp.float32

    part = pl.pallas_call(
        functools.partial(sums_kernel, shape, steps),
        out_shape=jax.ShapeDtypeStruct(cells, f32),
        grid=(steps,),
        in_specs=[smem, smem, solvent_spec, occupancy_spec, vmem, vmem, vmem],
        out_specs=vmem,
        scratch_shapes=[pltpu.VMEM((n_x + 1, 3 * rows + width_y, width_z), f32)],
        name="sums",
    )(grid_shift, colloid_count, solvent, occupancy, colloid_pos, colloid_vel, colloid_mass)

    fields, pos_out, vel_out = pl.pallas_call(
        functools.partial(exchange_kernel, shape),
        out_shape=[
            jax.ShapeDtypeStruct(cells, f32),
            jax.ShapeDtypeStruct(colloid_pos.shape, f32),
            jax.ShapeDtypeStruct(colloid_vel.shape, f32),
        ],
        in_specs=[smem, smem] + [vmem] * 5,
        out_specs=[vmem] * 3,
        scratch_shapes=[
            pltpu.VMEM((n_y, 8, width_z), f32),
            pltpu.VMEM((n_x, 8, width_z), f32),
            pltpu.VMEM((8, width_z), f32),
            pltpu.VMEM((n_y, 8, width_z), f32),
            pltpu.VMEM((n_x, 8, width_z), f32),
            pltpu.VMEM((8, width_z), f32),
            pltpu.VMEM((SUBSTEPS, 8, slots), f32),
            pltpu.VMEM((SUBSTEPS, 8, 8, slots), f32),
            pltpu.VMEM((3, slots, slots), f32),
            pltpu.VMEM((3, slots, slots), f32),
            pltpu.SemaphoreType.DMA((6,)),
            pltpu.SemaphoreType.DMA((6,)),
            pltpu.SemaphoreType.DMA((SUBSTEPS, 8)),
            pltpu.SemaphoreType.DMA((SUBSTEPS, 8)),
        ],
        compiler_params=pltpu.CompilerParams(collective_id=0, has_side_effects=True),
        name="exchange",
    )(grid_shift, colloid_count, part, axis_index, colloid_pos, colloid_vel, colloid_mass)

    solvent_out = pl.pallas_call(
        functools.partial(rotate_kernel, shape, steps),
        out_shape=jax.ShapeDtypeStruct(solvent.shape, f32),
        grid=(steps,),
        in_specs=[smem, solvent_spec, occupancy_spec, vmem],
        out_specs=solvent_spec,
        name="rotate",
    )(grid_shift, solvent, occupancy, fields)
    return (solvent_out.reshape(solvent_vel.shape), pos_out, vel_out)


def solution(mesh):
    return jax.shard_map(
        per_device,
        mesh=mesh,
        in_specs=(
            P(None, "gx", "yz", None, None),
            P("gx", "yz", None),
            P(),
            P("gx", "yz", None),
            P(None, "gx", "yz", None),
            P(None, "gx", "yz", None),
            P("gx", "yz", None),
            P("gx", "yz"),
        ),
        out_specs=(
            P(None, "gx", "yz", None, None),
            P(None, "gx", "yz", None),
            P(None, "gx", "yz", None),
        ),
        check_vma=False,
    )
```

profile of v0, /device:TPU:0, one launch (start us, length us, event | category | flops | bytes accessed | tf_op | source)
XLA Modules:
  0.0 46.6 jit_solution(11325791704925769138)
XLA Ops:
  1.3 5.2 %sums.1.part = f32[9,9,8,128]{3,2,1,0:T(8,128)} custom-call(s32[3]{0:T(128)} %shift.5, s32[1,1]{1,0:T(1,128)S(6)} %copy.13.count, f32[3,32,64,128]{3,2,1,0:T(8,128)} %bitcast.2, s32[32,32,128]{2,1,0:T(8,128)} %occupancy.3, f32[3,1,1,128]{3,2,1,0:T(1,128)} %pos.3, f32[3,1,1,128]{3,2,1,0:T(1,128)} %vel.3, f32[1,1,128]{2,1,0:T(1,128)} %mass.3), custom_call_target="tpu_custom_call" | custom-call | tf_op jit(solution)/shard_map/sums/pallas_call | solution.py:378
  6.5 32.1 %exchange.1 = (f32[9,9,8,128]{3,2,1,0:T(8,128)}, f32[3,1,1,128]{3,2,1,0:T(1,128)}, f32[3,1,1,128]{3,2,1,0:T(1,128)}) custom-call(s32[3]{0:T(128)} %shift.5, s32[1,1]{1,0:T(1,128)S(6)} %copy.13.count, f32[9,9,8,128]{3,2,1,0:T(8,128)} %sums.1.part, s32[8,8,64]{2,1,0:T(8,128)} %axis.1, f32[3,1,1,128]{3,2,1,0:T(1,128)} %pos.3, f32[3,1,1,128]{3,2,1,0:T(1,128)} %vel.3, ...), custom_call_target="tpu_custom_call" | custom-call | tf_op jit(solution)/shard_map/exchange/pallas_call | solution.py:388
  38.7 0.0 copy-start.1
  38.7 0.0 copy-start
  38.7 6.8 %rotate.1 = f32[3,32,64,128]{3,2,1,0:T(8,128)} custom-call(s32[3]{0:T(128)} %shift.5, f32[3,32,64,128]{3,2,1,0:T(8,128)} %bitcast.3, s32[32,32,128]{2,1,0:T(8,128)} %occupancy.3, f32[9,9,8,128]{3,2,1,0:T(8,128)} %get-tuple-element.6.fields), custom_call_target="tpu_custom_call" | custom-call | tf_op jit(solution)/shard_map/rotate/pallas_call | solution.py:417
  45.5 0.0 copy-done.1
  45.5 0.6 %copy.14 = f32[3,1,1,128]{3,2,1,0:T(1,128)} copy(f32[3,1,1,128]{3,2,1,0:T(1,128)S(1)} %copy-done.1) | data formatting | bytes 3072
  46.0 0.0 copy-done
  46.1 0.6 %copy.15 = f32[3,1,1,128]{3,2,1,0:T(1,128)} copy(f32[3,1,1,128]{3,2,1,0:T(1,128)S(1)} %copy-done) | data formatting | bytes 3072
Async XLA Ops:
  38.7 6.8 %copy-start.1 = (f32[3,1,1,128]{3,2,1,0:T(1,128)S(1)}, f32[3,1,1,128]{3,2,1,0:T(1,128)}, u32[]{:S(2)}) copy-start(f32[3,1,1,128]{3,2,1,0:T(1,128)} %get-tuple-element.13) | copy-start | bytes 4612
  38.7 7.4 %copy-start = (f32[3,1,1,128]{3,2,1,0:T(1,128)S(1)}, f32[3,1,1,128]{3,2,1,0:T(1,128)}, u32[]{:S(2)}) copy-start(f32[3,1,1,128]{3,2,1,0:T(1,128)} %get-tuple-element.14) | copy-start | bytes 4612
where the time goes:
time: 46.9 us; the launch traced here: 46.6 us
  Pallas kernels  44.2 us (94%)
  between operations  1.3 us (3%)
  local copies, waits for them, and re-layouts  1.13 us (2%)
    pallas_call x1, Pallas kernels, per_device(): pl.pallas_call(functools.partial(exchange_kernel, shape), out_shape=[jax....  32.1 us
    pallas_call x1, Pallas kernels, per_device(): pl.pallas_call(functools.partial(rotate_kernel, shape, steps), out_shape=...  6.8 us
    pallas_call x1, Pallas kernels, per_device(): pl.pallas_call(functools.partial(sums_kernel, shape, steps), out_shape=ja...  5.23 us
    unnamed x6, local copies, waits for them, and re-layouts  1.13 us

commit v1 on v0

v1 whole, which is shorter than its diff:
```python
import functools
import math

import jax
import jax.numpy as jnp
from jax import lax
from jax.experimental import pallas as pl
from jax.experimental.pallas import tpu as pltpu
from jax.sharding import PartitionSpec as P

CX = 8
CY = 8
CZ = 64
SUB = 4
SUBSTEPS = 4
DIRECTIONS = 64


turn_angle = 130.0 * math.pi / 180.0
cos_angle = math.cos(turn_angle)
sin_angle = math.sin(turn_angle)
golden = math.pi * (3.0 - math.sqrt(5.0))
cutoff = 1.5
stiffness = 20.0
timestep = 0.05
fill_mass = 16.0
MESH = pl.DeviceIdType.MESH


def iota(shape, dim):
    return lax.broadcasted_iota(jnp.int32, shape, dim)


def three_terms(value):
    high = value.astype(jnp.bfloat16)
    rest = value - high.astype(jnp.float32)
    middle = rest.astype(jnp.bfloat16)
    low = (rest - middle.astype(jnp.float32)).astype(jnp.bfloat16)
    return (high, middle, low)


def dot(left, right, contract=((1,), (0,))):
    return lax.dot_general(left, right, (contract, ((), ())), preferred_element_type=jnp.float32)


def wrapped(value, size):
    return jnp.where(value >= size, value - size, value)


def layer_of(row, scale, width):
    return jnp.clip(jnp.floor(row * scale).astype(jnp.int32), 0, width - 1)


def accumulate(shape, steps, shift_x, solvent, occupancy, acc):
    width_x, width_y, width_z = shape
    block_x = width_x // steps
    rows = 2 * width_y
    step = pl.program_id(0)

    @pl.when(step == 0)
    def _():
        acc[...] = jnp.zeros_like(acc)

    double = (iota((rows, width_y), 0) >> 1 == iota((rows, width_y), 1)).astype(jnp.bfloat16)
    slot = (iota((rows, width_z), 0) & 1).astype(jnp.float32)
    for first in range(0, block_x, SUB):
        cell = step * (block_x // SUB) + first // SUB
        filled = [occupancy[first + r].astype(jnp.float32) for r in range(SUB)]
        live = [dot(double, f.astype(jnp.bfloat16)) > slot for f in filled]
        for c in range(4):
            size = rows if c < 3 else width_y
            at = pl.ds(c * rows, size)
            near = jnp.zeros((size, width_z), jnp.float32)
            far = near
            for r in range(SUB):
                value = jnp.where(live[r], solvent[c, first + r], 0.0) if c < 3 else filled[r]
                stays = jnp.broadcast_to(shift_x + r, (size, width_z)) < SUB
                near = near + jnp.where(stays, value, 0.0)
                far = far + jnp.where(stays, 0.0, value)
            acc[cell, at, :] += near
            acc[cell + 1, at, :] += far


def cell_sums(shape, shift, count, pos, vel, mass, part, acc):
    width_x, width_y, width_z = shape
    cells_x, cells_y = (width_x // SUB + 1, width_y // SUB + 1)
    rows = 2 * width_y
    shift_x, shift_y, shift_z = (shift[0], shift[1], shift[2])
    total = 3 * rows + width_y
    column = iota((cells_y * 8, total), 1)
    target = iota((cells_y * 8, total), 0)
    heavy = column >= 3 * rows
    which = jnp.where(heavy, 3, (column >= rows).astype(jnp.int32) + (column >= 2 * rows).astype(jnp.int32))
    layer = jnp.where(heavy, column - 3 * rows, (column - which * rows) >> 1)
    fits = jnp.logical_and(which == (target & 7), ((layer + shift_y) >> 2) == (target >> 3))
    select = fits.astype(jnp.float32).astype(jnp.bfloat16)

    cell_x = (layer_of(pos[0, 0], SUB, width_x) + shift_x) >> 2
    cell_y = (layer_of(pos[1, 0], SUB, width_y) + shift_y) >> 2
    cell_z = wrapped(layer_of(pos[2, 0], 2.0, width_z) + shift_z, width_z) >> 1
    slots = mass.shape[2]
    alive = (iota((1, slots), 1) < count[0, 0]).astype(jnp.float32)
    weight = mass[0] * alive
    comp = iota((8, slots), 0)
    values = jnp.where(
        comp == 0,
        vel[0, 0] * weight,
        jnp.where(
            comp == 1,
            vel[1, 0] * weight,
            jnp.where(comp == 2, vel[2, 0] * weight, jnp.where(comp == 3, weight, 0.0)),
        ),
    )
    place = jnp.broadcast_to(cell_x * cells_y + cell_y, (8, slots))
    near = (wrapped(iota((width_z, slots), 0) + shift_z, width_z) >> 1) == cell_z
    near = near.astype(jnp.float32).astype(jnp.bfloat16)
    even = ((iota((cells_y * 8, width_z), 1) + shift_z) & 1) == 0
    for i in range(cells_x):
        sums = sum(dot(select, term) for term in three_terms(acc[i])[::-1])
        partner = jnp.where(
            even, pltpu.roll(sums, width_z - 1, 1), pltpu.roll(sums, 1, 1)
        )
        number = iota((cells_y, 8, slots), 0) + i * cells_y
        spread = jnp.where(number == place[None], values[None], 0.0).reshape(cells_y * 8, slots)
        deposit = sum(dot(term, near, ((1,), (1,))) for term in three_terms(spread)[::-1])
        part[i] = (sums + partner + deposit).reshape(cells_y, 8, width_z)


def exchange_kernel(
    shape, steps, shift, count, solvent, occupancy, axis, pos, vel, mass, fields, pos_out, vel_out,
    acc, part, halo_x, halo_y, halo_c, edge_x, edge_y, edge_c, sent, got, own, force,
    halo_sem, edge_sem, sent_sem, got_sem,
):
    width_x, width_y, width_z = shape
    n_x, n_y = (width_x // SUB, width_y // SUB)
    slots = mass.shape[2]
    me_x, me_y = (lax.axis_index("gx"), lax.axis_index("yz"))
    size_x, size_y = (lax.axis_size("gx"), lax.axis_size("yz"))
    shift_x, shift_y, shift_z = (shift[0], shift[1], shift[2])

    def device(a, b):
        return (lax.rem(me_x + a + size_x, size_x), lax.rem(me_y + b + size_y, size_y))

    around = [(a, b) for a in (-1, 0, 1) for b in (-1, 0, 1) if (a, b) != (0, 0)]
    barrier = pltpu.get_barrier_semaphore()
    grid_step = pl.program_id(0)

    @pl.when(grid_step == 0)
    def _():
        for a, b in around:
            pl.semaphore_signal(barrier, inc=1, device_id=device(a, b), device_id_type=MESH)

    accumulate(shape, steps, shift_x, solvent, occupancy, acc)

    @pl.when(grid_step == steps - 1)
    def _():
        alive = (iota((1, slots), 1) < count[0, 0]).astype(jnp.float32)
        comp = iota((8, slots), 0)

        def stacked(rows):
            out = jnp.zeros((8, slots), jnp.float32)
            for c, row in enumerate(rows):
                out = jnp.where(comp == c, row, out)
            return out

        def columns(rows):
            block = jnp.concatenate([rows, jnp.zeros((slots - 8, slots), jnp.float32)], axis=0)
            return block.T

        start_rows = stacked([pos[0, 0], pos[1, 0], pos[2, 0], alive, mass[0]])
        sent[0] = start_rows
        pl.semaphore_wait(barrier, len(around))

        def remote(src, dst, send, receive, where):
            return pltpu.make_async_remote_copy(
                src_ref=src, dst_ref=dst, send_sem=send, recv_sem=receive,
                device_id=where, device_id_type=MESH,
            )

        def exchange(step):
            copies = []
            for k, (a, b) in enumerate(around):
                copies.append(
                    remote(
                        sent.at[step], got.at[step, 7 - k],
                        sent_sem.at[step, k], got_sem.at[step, 7 - k], device(a, b),
                    )
                )
            for copy in copies:
                copy.start()
            return copies

        copies = exchange(0)

        cell_sums(shape, shift, count, pos, vel, mass, part, acc)
        halo = [
            remote(part.at[n_x, pl.ds(0, n_y)], halo_x, halo_sem.at[0], halo_sem.at[3], device(1, 0)),
            remote(part.at[pl.ds(0, n_x), n_y], halo_y, halo_sem.at[1], halo_sem.at[4], device(0, 1)),
            remote(part.at[n_x, n_y], halo_c, halo_sem.at[2], halo_sem.at[5], device(1, 1)),
        ]
        for copy in halo:
            copy.start()

        state = columns(start_rows)
        place = [state[:, c : c + 1] for c in range(3)]
        mass_column = state[:, 4:5]

        index = axis[...].reshape(n_x * n_y, width_z // 2).astype(jnp.float32).astype(jnp.bfloat16)
        cell_z = wrapped(iota((width_z // 2, width_z), 1) + shift_z, width_z) >> 1
        expand = (cell_z == iota((width_z // 2, width_z), 0)).astype(jnp.float32).astype(jnp.bfloat16)
        number = dot(index, expand)
        height = 1.0 - (2.0 * number + 1.0) / DIRECTIONS
        radius = jnp.sqrt(1.0 - height * height)
        phase = number * golden
        normal = [radius * jnp.cos(phase), radius * jnp.sin(phase), height]
        sub = iota((n_x * n_y, 8, width_z), 1)
        spread = [jnp.broadcast_to(n[:, None, :], (n_x * n_y, 8, width_z)) for n in normal]
        directions = jnp.where(sub == 3, spread[0], jnp.where(sub == 4, spread[1], spread[2]))
        fields[pl.ds(0, n_x), pl.ds(0, n_y)] = directions.reshape(n_x, n_y, 8, width_z)

        for copy in halo:
            copy.wait()
        sub = iota((n_y, 8, width_z), 1)
        for i in range(n_x):
            total = part[i, pl.ds(0, n_y)]
            first = halo_y[i][None]
            if i == 0:
                total = total + halo_x[...]
                first = first + halo_c[...][None]
            total = jnp.concatenate([total[:1] + first, total[1:]], axis=0)
            mean = total / jnp.maximum(total[:, 3:4, :], fill_mass)
            fields[i, pl.ds(0, n_y)] = jnp.where(sub < 3, mean, fields[i, pl.ds(0, n_y)])
        edges = [
            remote(fields.at[0, pl.ds(0, n_y)], edge_x, edge_sem.at[0], edge_sem.at[3], device(-1, 0)),
            remote(fields.at[pl.ds(0, n_x), 0], edge_y, edge_sem.at[1], edge_sem.at[4], device(0, -1)),
            remote(fields.at[0, 0], edge_c, edge_sem.at[2], edge_sem.at[5], device(-1, -1)),
        ]
        for copy in edges:
            copy.start()

        groups = [
            [(pair, k) for k, pair in enumerate(around) if 0 in pair],
            [(pair, k) for k, pair in enumerate(around) if 0 not in pair],
        ]
        wide = 32 if slots % 32 == 0 else 8

        def forces(step, copies, place):
            for c in range(3):
                own[c] = jnp.broadcast_to(place[c], (slots, slots))

            for sources in [[((0, 0), None)]] + groups:
                for _, k in sources:
                    if k is not None:
                        copies[7 - k].wait_recv()

                def block(r, carry, sources=sources):
                    at = pl.ds(pl.multiple_of(r * wide, 8), wide)
                    own_x, own_y, own_z = (own[0, at, :], own[1, at, :], own[2, at, :])
                    total = None
                    for (a, b), k in sources:
                        def row(c):
                            if k is None:
                                return sent[step, pl.ds(c, 1), :]
                            return got[step, k, pl.ds(c, 1), :]

                        diff_x = own_x - (row(0) + float(a * CX))
                        diff_y = own_y - (row(1) + float(b * CY))
                        high = own_z - row(2)
                        high = jnp.where(
                            high > 0.5 * CZ, high - CZ, jnp.where(high < -0.5 * CZ, high + CZ, high)
                        )
                        radius_sq = diff_x * diff_x + diff_y * diff_y + high * high
                        reach = 1.0 - radius_sq * (1.0 / (cutoff * cutoff))
                        weight = jnp.where(radius_sq < cutoff * cutoff, reach * reach, 0.0) * row(3)
                        parts = [weight * diff_x, weight * diff_y, weight * high]
                        total = parts if total is None else [total[c] + parts[c] for c in range(3)]
                    for c in range(3):
                        if sources[0][1] is None:
                            force[c, at, :] = total[c]
                        else:
                            force[c, at, :] += total[c]
                    return carry

                lax.fori_loop(0, slots // wide, block, 0)
            for copy in copies:
                copy.wait_send()
            return [stiffness * jnp.sum(force[c], axis=1, keepdims=True) for c in range(3)]

        push = forces(0, copies, place)

        for copy in edges:
            copy.wait()
        fields[n_x, pl.ds(0, n_y)] = edge_x[...]
        fields[pl.ds(0, n_x), n_y] = edge_y[...]
        fields[n_x, n_y] = edge_c[...]

        layer_z = layer_of(pos[2, 0], 2.0, width_z)
        cell_x = (layer_of(pos[0, 0], SUB, width_x) + shift_x) >> 2
        cell_y = (layer_of(pos[1, 0], SUB, width_y) + shift_y) >> 2
        target = jnp.broadcast_to(cell_x * (n_y + 1) + cell_y, (8, slots))
        chosen = (iota((width_z, slots), 0) == layer_z).astype(jnp.float32).astype(jnp.bfloat16)
        picked = jnp.zeros((8, slots), jnp.float32)
        for i in range(n_x + 1):
            rows = fields[i].reshape((n_y + 1) * 8, width_z)
            at_z = sum(dot(term, chosen) for term in three_terms(rows)[::-1])
            number = iota((n_y + 1, 8, slots), 0) + i * (n_y + 1)
            at_z = at_z.reshape(n_y + 1, 8, slots)
            picked = picked + jnp.sum(jnp.where(number == target[None], at_z, 0.0), axis=0)
        mean = [picked[c : c + 1] for c in range(3)]
        n = [picked[c : c + 1] for c in range(3, 6)]
        rel = [vel[c, 0] - mean[c] for c in range(3)]
        cross = [n[1] * rel[2] - n[2] * rel[1], n[2] * rel[0] - n[0] * rel[2], n[0] * rel[1] - n[1] * rel[0]]
        along = n[0] * rel[0] + n[1] * rel[1] + n[2] * rel[2]
        turned = [
            mean[c] + cos_angle * rel[c] + sin_angle * cross[c] + (1.0 - cos_angle) * along * n[c]
            for c in range(3)
        ]
        state = columns(stacked([jnp.where(alive > 0, turned[c], vel[c, 0]) for c in range(3)]))
        speed = [state[:, c : c + 1] for c in range(3)]

        lane = iota((slots, slots), 1)
        for step in range(SUBSTEPS):
            speed = [speed[c] + timestep * push[c] / mass_column for c in range(3)]
            place = [place[c] + timestep * speed[c] for c in range(3)]
            block = jnp.zeros((slots, slots), jnp.float32)
            for c, column in enumerate(place):
                block = jnp.where(lane == c, column, block)
            if step == SUBSTEPS - 1:
                for c, column in enumerate(speed):
                    block = jnp.where(lane == 3 + c, column, block)
            flipped = block.T[:8]
            if step < SUBSTEPS - 1:
                sent[step + 1] = jnp.where(comp == 3, alive, flipped)
                copies = exchange(step + 1)
                push = forces(step + 1, copies, place)
        for c in range(3):
            pos_out[c, 0] = jnp.where(alive > 0, flipped[c : c + 1], pos[c, 0])
            vel_out[c, 0] = jnp.where(alive > 0, flipped[3 + c : 4 + c], vel[c, 0])


def rotate_kernel(shape, steps, shift, solvent, occupancy, fields, pos, vel, out, pos_out, vel_out):
    width_x, width_y, width_z = shape
    block_x = width_x // steps
    n_y = width_y // SUB
    rows = 2 * width_y
    step = pl.program_id(0)
    shift_x, shift_y = (shift[0], shift[1])
    double = (iota((rows, width_y), 0) >> 1 == iota((rows, width_y), 1)).astype(jnp.bfloat16)
    row = iota((8, width_z), 0)
    slot = (row & 1).astype(jnp.float32)
    later = ((row >> 1) + shift_y) >= SUB

    @pl.when(step == 0)
    def _():
        pos_out[...] = pos[...]
        vel_out[...] = vel[...]

    def layer(x, carry):
        held = dot(double, occupancy[x].astype(jnp.float32).astype(jnp.bfloat16))
        cell = (step * block_x + x + shift_x) >> 2
        for b in range(n_y):
            at = pl.ds(8 * b, 8)
            both = [
                jnp.where(
                    later, fields[cell, b + 1, pl.ds(c, 1), :], fields[cell, b, pl.ds(c, 1), :]
                )
                for c in range(6)
            ]
            mean, n = (both[:3], both[3:])
            old = [solvent[c, x, at, :] for c in range(3)]
            rel = [old[c] - mean[c] for c in range(3)]
            along = (1.0 - cos_angle) * (n[0] * rel[0] + n[1] * rel[1] + n[2] * rel[2])
            cross = [
                n[1] * rel[2] - n[2] * rel[1],
                n[2] * rel[0] - n[0] * rel[2],
                n[0] * rel[1] - n[1] * rel[0],
            ]
            live = held[8 * b : 8 * b + 8] > slot
            for c in range(3):
                new = mean[c] + cos_angle * rel[c] + sin_angle * cross[c] + along * n[c]
                out[c, x, at, :] = jnp.where(live, new, old[c])
        return carry

    lax.fori_loop(0, block_x, layer, 0)


def per_device(
    solvent_vel,
    occupancy,
    grid_shift,
    axis_index,
    colloid_pos,
    colloid_vel,
    colloid_mass,
    colloid_count,
):
    shape = occupancy.shape
    width_x, width_y, width_z = shape
    rows = 2 * width_y
    n_x, n_y = (width_x // SUB, width_y // SUB)
    slots = colloid_mass.shape[2]
    steps = 4
    block_x = width_x // steps
    solvent = solvent_vel.reshape(3, width_x, rows, width_z)
    smem = pl.BlockSpec(memory_space=pltpu.SMEM)
    vmem = pl.BlockSpec(memory_space=pltpu.VMEM)
    solvent_spec = pl.BlockSpec((3, block_x, rows, width_z), lambda i: (0, i, 0, 0))
    occupancy_spec = pl.BlockSpec((block_x, width_y, width_z), lambda i: (i, 0, 0))
    cells = (n_x + 1, n_y + 1, 8, width_z)
    f32 = jnp.float32

    fields, pos_out, vel_out = pl.pallas_call(
        functools.partial(exchange_kernel, shape, steps),
        grid=(steps,),
        out_shape=[
            jax.ShapeDtypeStruct(cells, f32),
            jax.ShapeDtypeStruct(colloid_pos.shape, f32),
            jax.ShapeDtypeStruct(colloid_vel.shape, f32),
        ],
        in_specs=[smem, smem, solvent_spec, occupancy_spec] + [vmem] * 4,
        out_specs=[vmem] * 3,
        scratch_shapes=[
            pltpu.VMEM((n_x + 1, 3 * rows + width_y, width_z), f32),
            pltpu.VMEM(cells, f32),
            pltpu.VMEM((n_y, 8, width_z), f32),
            pltpu.VMEM((n_x, 8, width_z), f32),
            pltpu.VMEM((8, width_z), f32),
            pltpu.VMEM((n_y, 8, width_z), f32),
            pltpu.VMEM((n_x, 8, width_z), f32),
            pltpu.VMEM((8, width_z), f32),
            pltpu.VMEM((SUBSTEPS, 8, slots), f32),
            pltpu.VMEM((SUBSTEPS, 8, 8, slots), f32),
            pltpu.VMEM((3, slots, slots), f32),
            pltpu.VMEM((3, slots, slots), f32),
            pltpu.SemaphoreType.DMA((6,)),
            pltpu.SemaphoreType.DMA((6,)),
            pltpu.SemaphoreType.DMA((SUBSTEPS, 8)),
            pltpu.SemaphoreType.DMA((SUBSTEPS, 8)),
        ],
        compiler_params=pltpu.CompilerParams(collective_id=0, has_side_effects=True),
        name="exchange",
    )(grid_shift, colloid_count, solvent, occupancy, axis_index, colloid_pos, colloid_vel, colloid_mass)

    turns = 8 if width_x % 8 == 0 else steps
    thin = width_x // turns
    solvent_spec = pl.BlockSpec((3, thin, rows, width_z), lambda i: (0, i, 0, 0))
    occupancy_spec = pl.BlockSpec((thin, width_y, width_z), lambda i: (i, 0, 0))
    solvent_out, pos_out, vel_out = pl.pallas_call(
        functools.partial(rotate_kernel, shape, turns),
        out_shape=[
            jax.ShapeDtypeStruct(solvent.shape, f32),
            jax.ShapeDtypeStruct(colloid_pos.shape, f32),
            jax.ShapeDtypeStruct(colloid_vel.shape, f32),
        ],
        grid=(turns,),
        in_specs=[smem, solvent_spec, occupancy_spec, vmem, vmem, vmem],
        out_specs=[solvent_spec, vmem, vmem],
        name="rotate",
    )(grid_shift, solvent, occupancy, fields, pos_out, vel_out)
    return (solvent_out.reshape(solvent_vel.shape), pos_out, vel_out)


def solution(mesh):
    return jax.shard_map(
        per_device,
        mesh=mesh,
        in_specs=(
            P(None, "gx", "yz", None, None),
            P("gx", "yz", None),
            P(),
            P("gx", "yz", None),
            P(None, "gx", "yz", None),
            P(None, "gx", "yz", None),
            P("gx", "yz", None),
            P("gx", "yz"),
        ),
        out_specs=(
            P(None, "gx", "yz", None, None),
            P(None, "gx", "yz", None),
            P(None, "gx", "yz", None),
        ),
        check_vma=False,
    )
```

time: 46.9 us -> 43.9 us (0.936)
  Pallas kernels: 44.2 us -> 42.3 us
  local copies, waits for them, and re-layouts: 1.13 us -> 0 us
    pallas_call x3 -> x2, Pallas kernels: 44.2 us -> 42.3 us  [the longest x1 34.1 us: per_device(): pl.pallas_call(functools.partial(exchange_kernel, shape, steps), grid=(st...]
    unnamed x6 -> x0, local copies, waits for them, and re-layouts: 1.13 us -> none
where the time goes in v1:
time: 43.9 us; the launch traced here: 43.5 us
  Pallas kernels  42.3 us (96%)
  between operations  1.29 us (3%)
    pallas_call x1, Pallas kernels, per_device(): pl.pallas_call(functools.partial(exchange_kernel, shape, steps), grid=(st...  34.1 us
    pallas_call x1, Pallas kernels, per_device(): pl.pallas_call(functools.partial(rotate_kernel, shape, turns), out_shape=...  8.2 us

profile of v1, /device:TPU:0, one launch (start us, length us, event | category | flops | bytes accessed | tf_op | source)
XLA Modules:
  0.0 43.5 jit_solution(15022659139647083848)
XLA Ops:
  1.3 34.1 %exchange.1 = (f32[9,9,8,128]{3,2,1,0:T(8,128)}, f32[3,1,1,128]{3,2,1,0:T(1,128)}, f32[3,1,1,128]{3,2,1,0:T(1,128)}) custom-call(s32[3]{0:T(128)} %shift.3, s32[1,1]{1,0:T(1,128)S(6)} %copy.11.count, f32[3,32,64,128]{3,2,1,0:T(8,128)} %bitcast.2, s32[32,32,128]{2,1,0:T(8,128)} %occupancy.3, s32[8,8,64]{2,1,0:T(8,128)} %axis.1, f32[3,1,1,128]{3,2,1,0:T(1,128)} %pos.1, ...), custom_call_target="tpu_custom_call" | custom-call | tf_op jit(solution)/shard_map/exchange/pallas_call | solution.py:412
  35.3 8.2 %rotate.1 = (f32[3,32,64,128]{3,2,1,0:T(8,128)}, f32[3,1,1,128]{3,2,1,0:T(1,128)}, f32[3,1,1,128]{3,2,1,0:T(1,128)}) custom-call(s32[3]{0:T(128)} %shift.3, f32[3,32,64,128]{3,2,1,0:T(8,128)} %bitcast.3, s32[32,32,128]{2,1,0:T(8,128)} %occupancy.3, f32[9,9,8,128]{3,2,1,0:T(8,128)} %get-tuple-element.9.fields, f32[3,1,1,128]{3,2,1,0:T(1,128)} %get-tuple-element.10.pos, ...), custom_call_target="tpu_custom_call" | custom-call | tf_op jit(solution)/shard_map/rotate/pallas_call | solution.py:448
